TPU v7x, 256 devices: a whole 4x4x8 slice. The times are simulated.
256 devices in a mesh: tm: 16 (over z, core), space: 16 (over y, x).
Axes of the slice: x: 4, y: 4, z: 8, core: 2. Of those that a mesh axis runs over, the one named last changes fastest.
Arguments:
- initial: float32 [2, 512, 512], P(None, 'space'), may hold values from 0.2 to 1
- guess: float32 [256, 2, 512, 512], P('tm', None, 'space'), may hold values from 0 to 1
- kappa: float32 [2, 512, 512], P(None, 'space'), may hold values from 0.005 to 0.05
- feed: float32 [512, 512], P('space'), may hold values from 0.002 to 0.01
- kill: float32 [512, 512], P('space'), may hold values from 0.002 to 0.008
- react: float32 [512, 512], P('space'), may hold values from 0.002 to 0.008
Outputs:
- solution: float32 [256, 2, 512, 512], P('tm', None, 'space')
All inputs are finite; a program needn't handle non-finite values.
Results may differ from a plain program's by a relative error of at most 0.00002.
Values sent between devices are 32-bit elements; how exact they have to be, the bound alone decides.
No kernel may reach another device: no remote copies, remote signals or barrier semaphores. Data moves between devices by JAX's collectives and lax.ppermute only.
A program may use at most 128 MiB of HBM per device.

v0:
```python
import jax
import jax.numpy as jnp
from jax import lax
from jax.sharding import Mesh
from jax.sharding import PartitionSpec as P

SPAN = 8
SPACE = ("space_0", "space_1")
TM = ("tm_0", "tm_1")
TM_SPACE = ("tm_0", "tm_1", "space_0", "space_1")


def padded_2(block, sides, width):
    for axis, dim in sides:
        count = lax.axis_size(axis)
        forward = [(i, i + 1) for i in range(count - 1)]
        backward = [(target, source) for source, target in forward]
        low = lax.ppermute(
            lax.slice_in_dim(block, block.shape[dim] - width, None, axis=dim), axis, forward
        )
        high = lax.ppermute(lax.slice_in_dim(block, 0, width, axis=dim), axis, backward)
        block = jnp.concatenate([low, block, high], axis=dim)
    return block


def shifted(block, axis, distance):
    devices = range(lax.axis_size(axis))
    route = [(i - distance, i) for i in devices if i - distance in devices]
    return lax.ppermute(block, axis, route)


def in_order(parts, dim):
    shape = list(parts.shape[1:])
    shape[dim] *= parts.shape[0]
    return jnp.moveaxis(parts, 0, dim).reshape(shape)


def gather_in_order(x, axes, turns):
    parts = x[None]
    for k in turns:
        parts = lax.all_gather(parts, axes[k], axis=0, tiled=True)
    carried = [lax.axis_size(axes[k]) for k in reversed(turns)]
    parts = parts.reshape(*carried, *x.shape)
    turned = sorted(range(len(turns)), key=lambda place: turns[len(turns) - 1 - place])
    return parts.transpose(*turned, *range(len(turns), parts.ndim)).reshape(-1, *x.shape)


def gather_axes(x, axes, turns, dim):
    return in_order(gather_in_order(x, axes, turns), dim)


def coarsen(field):
    shape = field.shape
    blocks = field.reshape(shape[:-2] + (shape[-2] // 2, 2, shape[-1] // 2, 2))
    return blocks.mean(axis=(-3, -1))


def refine(field):
    return jnp.repeat(jnp.repeat(field, 2, axis=-2), 2, axis=-1)


def advance(state, row_padded, coeffs):
    spread, supply, removal, coupling = coeffs
    padded = jnp.pad(row_padded, [(0, 0)] * (row_padded.ndim - 1) + [(1, 1)])
    laplace = (
        padded[..., :-2, 1:-1]
        + padded[..., 2:, 1:-1]
        + padded[..., 1:-1, :-2]
        + padded[..., 1:-1, 2:]
        - 4.0 * state
    )
    first_species = state[..., 0, :, :]
    second_species = state[..., 1, :, :]
    coupled = coupling * first_species * second_species * second_species
    next_first = (
        first_species + spread[0] * laplace[..., 0, :, :] - coupled + supply * (1.0 - first_species)
    )
    next_second = (
        second_species
        + spread[1] * laplace[..., 1, :, :]
        + coupled
        - (supply + removal) * second_species
    )
    return jnp.stack([next_first, next_second], axis=-3)


def margin_advance(state, coeffs, inside_mask):
    row_padded = jnp.pad(state, [(0, 0)] * (state.ndim - 2) + [(1, 1), (0, 0)])
    return advance(state, row_padded, coeffs) * inside_mask


def inside_rows(strip_rows, margin):
    global_rows = (
        lax.axis_index(SPACE) * strip_rows
        - margin
        + jnp.arange(strip_rows + 2 * margin, dtype=jnp.int32)
    )
    inside_mask = (global_rows >= 0) & (global_rows < strip_rows * lax.axis_size(SPACE))
    return inside_mask.astype(jnp.float32)[:, None]


def split_coeffs(packed):
    return (packed[0:2], packed[2], packed[3], packed[4])


def pack_coeffs(coeffs):
    return jnp.concatenate([coeffs[0], coeffs[1][None], coeffs[2][None], coeffs[3][None]])


def local(initial, guess, kappa, feed, kill, react):
    group = SPAN // 2
    time_index = lax.axis_index(TM)
    opening = time_index == 0
    member = time_index % group
    holder = member == group - 1
    level_zero = (kappa, feed, kill, react)
    spread_one = coarsen(kappa)
    supply_one = coarsen(feed)
    removal_one = coarsen(kill)
    coupling_one = coarsen(react)
    level_one = (2.0 * spread_one, 8.0 * supply_one, 8.0 * removal_one, 8.0 * coupling_one)
    level_two = (
        4.0 * coarsen(spread_one),
        64.0 * coarsen(supply_one),
        64.0 * coarsen(removal_one),
        64.0 * coarsen(coupling_one),
    )
    start_one = coarsen(initial)
    start_two = coarsen(start_one)
    strip_rows = initial.shape[-2]
    mid_rows = strip_rows // 2
    margin = SPAN - 1

    def fine_step(state):
        row_padded = padded_2(state, ((SPACE, 2),), 1)
        return advance(state, row_padded, level_zero)

    def fine_relax(series):
        incoming = shifted(series[-1], TM, 1)
        incoming = jnp.where(opening, initial, incoming)
        current = jnp.stack([incoming, series[SPAN - 1]])
        early = []
        later = []
        widened = padded_2(current, ((SPACE, 2),), margin)
        for position in range(SPAN - 1):
            widened = margin_advance(widened, fine_wide_coeffs, fine_mask)
            early.append(widened[0, :, margin : margin + strip_rows])
            later.append(widened[1, :, margin : margin + strip_rows])
        return (jnp.stack(early + [series[SPAN - 1]] + later + [series[-1]]), incoming)

    def mid_relax(values):
        predicted = values[1]
        for section in range(group):
            incoming = shifted(values[1], TM, 1)
            incoming = jnp.where(opening, start_one, incoming)
            widened = padded_2(incoming, ((SPACE, 1),), 2)
            first_wide = margin_advance(widened, mid_wide_coeffs, mid_mask) + mid_wide_forcing[0]
            second_wide = (
                margin_advance(first_wide, mid_wide_coeffs, mid_mask) + mid_wide_forcing[1]
            )
            fresh_first = first_wide[:, 2 : 2 + mid_rows]
            predicted = second_wide[:, 2 : 2 + mid_rows]
            fresh_second = predicted if section < group - 1 else values[1]
            values = jnp.where(member == section, jnp.stack([fresh_first, fresh_second]), values)
        return (values, predicted)

    fine_wide = padded_2(pack_coeffs(level_zero), ((SPACE, 1),), margin)
    fine_wide_coeffs = split_coeffs(fine_wide)
    fine_mask = inside_rows(strip_rows, margin)
    mid_mask = inside_rows(mid_rows, 2)
    series, incoming = fine_relax(guess)
    updated = fine_step(jnp.stack([series[SPAN - 2], series[-2]]))
    series = series.at[SPAN - 1].set(updated[0]).at[-1].set(updated[1])
    series, incoming = fine_relax(series)
    ends = jnp.stack([series[SPAN - 1], series[-1]])
    residual = fine_step(jnp.stack([series[SPAN - 2], series[-2]])) - ends
    restricted = coarsen(ends)
    earlier = jnp.stack([coarsen(incoming), restricted[0]])
    row_padded = padded_2(earlier, ((SPACE, 2),), 1)
    forcing_one = coarsen(residual) + restricted - advance(earlier, row_padded, level_one)
    mid_packed = jnp.concatenate(
        [pack_coeffs(level_one), forcing_one.reshape((4,) + forcing_one.shape[-2:])]
    )
    mid_wide = padded_2(mid_packed, ((SPACE, 1),), 2)
    mid_wide_coeffs = split_coeffs(mid_wide)
    mid_wide_forcing = mid_wide[5:9].reshape((2, 2) + mid_wide.shape[-2:])
    middle, predicted = mid_relax(restricted)
    coarse_values = coarsen(middle[1])
    coarse_right = coarsen(predicted - middle[1]) + coarse_values
    tm_count = lax.axis_size(TM)
    space_count = lax.axis_size(SPACE)
    rows_two = coarse_values.shape[-2]
    cols_two = coarse_values.shape[-1]
    quarter = cols_two // group
    reach = tm_count // group
    stacked = jnp.concatenate([coarse_values, coarse_right])
    held_piece = stacked[..., (group - 1) * quarter :]
    for distance in range(1, group):
        sent_part = stacked[..., (group - 1 - distance) * quarter : (group - distance) * quarter]
        arriving = shifted(sent_part, TM, -distance)
        held_piece = jnp.where(member == group - 1 - distance, arriving, held_piece)
    gathered = gather_axes(held_piece[None], TM_SPACE, (0, 2, 3, 1), 0)
    arranged = gathered.reshape((tm_count // group, group, space_count, 4, rows_two, quarter))
    arranged = jnp.transpose(arranged, (0, 3, 2, 4, 1, 5)).reshape(
        (tm_count // group, 4, space_count * rows_two, cols_two)
    )
    padded_held = jnp.pad(arranged, ((0, 0), (0, 0), (reach, reach), (0, 0)))
    window = lax.dynamic_slice_in_dim(
        padded_held, lax.axis_index(SPACE) * rows_two, rows_two + 2 * reach, 2
    )
    held_values = window[:, 0:2]
    held_right = window[:, 2:4]
    packed = jnp.concatenate([pack_coeffs(level_two), start_two])
    widened = padded_2(packed, ((SPACE, 1),), reach)
    wide_coeffs = split_coeffs(widened)
    wide_start = widened[5:7]
    coarse_mask = inside_rows(rows_two, reach)

    def wide_step(state):
        return margin_advance(state, wide_coeffs, coarse_mask)

    coarse_prev = jnp.concatenate([wide_start[None], held_values[:-1]])
    forcing_two = held_right - wide_step(coarse_prev)

    def march(previous, forcing_step):
        following = wide_step(previous) + forcing_step
        return (following, following)

    unused, solved = lax.scan(march, wide_start, forcing_two)
    own_point = time_index // group
    wide_change = lax.dynamic_index_in_dim(solved, own_point, 0, False) - lax.dynamic_index_in_dim(
        held_values, own_point, 0, False
    )
    correction = wide_change[:, reach : reach + rows_two]
    middle = middle.at[1].set(jnp.where(holder, middle[1] + refine(correction), middle[1]))
    middle, predicted = mid_relax(middle)
    change = refine(middle - restricted)
    series = series.at[SPAN - 1].add(change[0]).at[-1].add(change[1])
    series, incoming = fine_relax(series)
    return series


def solution(mesh):
    split = Mesh(mesh.devices.reshape(8, 2, 4, 4), ("tm_0", "tm_1", "space_0", "space_1"))
    placed = (
        P(None, SPACE, None),
        P(TM, None, SPACE, None),
        P(None, SPACE, None),
        P(SPACE, None),
        P(SPACE, None),
        P(SPACE, None),
    )
    return jax.shard_map(
        local, mesh=split, in_specs=placed, out_specs=P(TM, None, SPACE, None), check_vma=False
    )
```

profile of v0, /device:TPU:134, one launch (start us, length us, event | category | flops | bytes accessed | tf_op | source)
XLA Modules:
  0.0 520.0 jit_solution(8484025513956494548)
XLA Ops:
  17.1 6.4 %reshape.425 = f32[16,2,256,2]{3,2,1,0:T(8,128)} reshape(f32[32,512]{1,0:T(8,128)} %param.21) | data formatting | bytes 131072 | tf_op jit(solution)/shard_map/reshape | solution.py:54
  23.5 5.5 %reshape.426 = f32[16,2,256,2]{3,2,1,0:T(8,128)} reshape(f32[32,512]{1,0:T(8,128)S(1)} %copy-done.4) | data formatting | bytes 131072 | tf_op jit(solution)/shard_map/reshape | solution.py:54
  29.1 5.6 %reshape.427 = f32[16,2,256,2]{3,2,1,0:T(8,128)} reshape(f32[32,512]{1,0:T(8,128)S(1)} %copy-done.3) | data formatting | bytes 131072 | tf_op jit(solution)/shard_map/reshape | solution.py:54
  34.6 9.8 %reshape.424 = f32[2,16,2,256,2]{4,3,2,1,0:T(8,128)} reshape(f32[2,32,512]{2,1,0:T(8,128)S(1)} %copy-done.1) | data formatting | bytes 262144 | tf_op jit(solution)/shard_map/reshape | solution.py:54
  57.8 5.5 %collective-permute-start.1 = (f32[2,2,7,512]{3,1,2,0:T(2,128)S(1)}, f32[2,2,7,512]{3,1,2,0:T(2,128)S(1)}, u32[]{:S(2)}, u32[]{:S(2)}) collective-permute-start(f32[2,2,7,512]{3,1,2,0:T(2,128)S(1)} %copy.483), channel_id=1, source_target_pairs={{0,1},{1,2},{2,3},{3,4},{4,5},{5,6},{6,7},{7,8},{8,9},{9,10},{10,1... | collective-permute-start | bytes 172040 | tf_op jit(solution)/shard_map/ppermute | solution.py:18
  65.6 6.0 %collective-permute-done.2 = f32[2,2,7,512]{3,1,2,0:T(2,128)S(1)} collective-permute-done((f32[2,2,7,512]{3,1,2,0:T(2,128)S(1)}, f32[2,2,7,512]{3,1,2,0:T(2,128)S(1)}, u32[]{:S(2)}, u32[]{:S(2)}) %collective-permute-start.2) | collective-permute-done | bytes 57376 | tf_op jit(solution)/shard_map/ppermute | solution.py:21
  81.7 9.8 %reshape.422 = f32[2,16,2,256,2]{4,3,2,1,0:T(8,128)} reshape(f32[2,32,512]{2,1,0:T(8,128)S(1)} %copy-done.2) | data formatting | bytes 262144 | tf_op jit(solution)/shard_map/reshape | solution.py:54
  96.7 18.1 %reshape.423 = f32[2,2,16,2,256,2]{5,4,3,2,1,0:T(8,128)} reshape(f32[2,2,32,512]{3,2,1,0:T(8,128)S(1)} %pad_maximum_fusion.4) | data formatting | bytes 524288 | tf_op jit(solution)/shard_map/reshape | solution.py:54
  114.8 8.0 %reduce_sum.136 = f32[2,2,16,256]{3,2,1,0:T(8,128)S(1)} reduce(f32[2,2,16,2,256,2]{5,4,3,2,1,0:T(8,128)} %reshape.423, f32[]{:T(128)} %constant.259.clone.1), dimensions={3,5}, to_apply=%region_1.2 | reduce | flops 49152 | bytes 327684 | tf_op jit(solution)/shard_map/reduce_sum | solution.py:55
  135.8 9.8 %stack.349 = f32[1,2,16,2,256,2]{5,4,3,2,1,0:T(8,128)} reshape(f32[1,2,32,512]{3,2,1,0:T(8,128)S(1)} %get-tuple-element.295) | data formatting | bytes 262144 | tf_op jit(solution)/shard_map/stack | solution.py:175
  145.6 9.7 %stack.348 = f32[1,2,16,2,256,2]{5,4,3,2,1,0:T(8,128)} reshape(f32[1,2,32,512]{3,2,1,0:T(8,128)S(1)} %get-tuple-element.296) | data formatting | bytes 262144 | tf_op jit(solution)/shard_map/stack | solution.py:175
  155.3 5.2 %copy.505 = f32[1,2,16,2,256,2]{4,2,5,3,1,0:T(8,128)S(1)} copy(f32[1,2,16,2,256,2]{5,4,3,2,1,0:T(8,128)} %stack.348) | data formatting | bytes 262144 | tf_op jit(solution)/shard_map/stack | solution.py:175
  160.5 5.2 %copy.506 = f32[1,2,16,2,256,2]{4,2,5,3,1,0:T(8,128)S(1)} copy(f32[1,2,16,2,256,2]{5,4,3,2,1,0:T(8,128)} %stack.349) | data formatting | bytes 262144 | tf_op jit(solution)/shard_map/stack | solution.py:175
  165.8 9.8 %reshape.428 = f32[2,16,2,256,2]{4,3,2,1,0:T(8,128)} reshape(f32[2,32,512]{2,1,0:T(8,128)S(1)} %broadcast_select_fusion) | data formatting | bytes 262144 | tf_op jit(solution)/shard_map/reshape | solution.py:54
  180.2 6.0 %collective-permute-start.15 = (f32[2,2,1,256]{3,2,1,0:T(1,128)S(1)}, f32[2,2,1,256]{3,2,1,0:T(1,128)S(1)}, u32[]{:S(2)}, u32[]{:S(2)}) collective-permute-start(f32[2,2,1,256]{3,2,1,0:T(1,128)S(1)} %get-tuple-element.342), channel_id=1, source_target_pairs={{0,1},{1,2},{2,3},{3,4},{4,5},{5,6},{6,7},{7,8},{8,9},{9,10},{10,1... | collective-permute-start | bytes 12296 | tf_op jit(solution)/shard_map/ppermute | solution.py:18
  188.3 6.0 %collective-permute-start.11 = (f32[2,2,7,512]{3,1,2,0:T(2,128)S(1)}, f32[2,2,7,512]{3,1,2,0:T(2,128)S(1)}, u32[]{:S(2)}, u32[]{:S(2)}) collective-permute-start(f32[2,2,7,512]{3,1,2,0:T(2,128)S(1)} %copy.493), channel_id=1, source_target_pairs={{0,1},{1,2},{2,3},{3,4},{4,5},{5,6},{6,7},{7,8},{8,9},{9,10},{10,1... | collective-permute-start | bytes 172040 | tf_op jit(solution)/shard_map/ppermute | solution.py:18
  196.6 6.0 %collective-permute-done.12 = f32[2,2,7,512]{3,1,2,0:T(2,128)S(1)} collective-permute-done((f32[2,2,7,512]{3,1,2,0:T(2,128)S(1)}, f32[2,2,7,512]{3,1,2,0:T(2,128)S(1)}, u32[]{:S(2)}, u32[]{:S(2)}) %collective-permute-start.12) | collective-permute-done | bytes 57376 | tf_op jit(solution)/shard_map/ppermute | solution.py:21
  216.9 9.8 %stack.345 = f32[2,1,16,2,256,2]{5,4,3,2,0,1:T(8,128)} reshape(f32[2,1,32,512]{3,2,1,0:T(8,128)S(1)} %get-tuple-element.276) | data formatting | bytes 262144 | tf_op jit(solution)/shard_map/stack | solution.py:84
  226.7 5.2 %copy.503 = f32[2,1,16,2,256,2]{4,2,5,3,1,0:T(8,128)S(1)} copy(f32[2,1,16,2,256,2]{5,4,3,2,0,1:T(8,128)} %stack.345) | data formatting | bytes 262144 | tf_op jit(solution)/shard_map/stack | solution.py:84
  231.9 9.8 %stack.346 = f32[2,1,16,2,256,2]{5,4,3,2,0,1:T(8,128)} reshape(f32[2,1,32,512]{3,2,1,0:T(8,128)S(1)} %get-tuple-element.277) | data formatting | bytes 262144 | tf_op jit(solution)/shard_map/stack | solution.py:84
  329.6 25.1 %all-gather = f32[32,8,32]{2,1,0:T(8,128)S(1)} all-gather(f32[4,8,32]{2,1,0:T(8,128)S(1)} %fusion.421), channel_id=2, replica_groups=mesh['tm_0'=8,'tm_1'=2,'space_0'=4,'space_1'=4] {'tm_0'}, dimensions={0}, use_global_device_ids=true | all-gather | bytes 36864 | tf_op jit(solution)/shard_map/all_gather | solution.py:41
  354.7 13.0 %all_gather.13 = f32[32,1,4,8,32]{4,3,2,1,0:T(8,128)S(1)} all-gather(f32[8,1,4,8,32]{4,3,2,1,0:T(8,128)S(1)} %bitcast.180), channel_id=1, replica_groups=mesh['tm_0'=8,'tm_1'=2,'space_0'=4,'space_1'=4] {'space_0'}, dimensions={0}, use_global_device_ids=true | all-gather | bytes 163840 | tf_op jit(solution)/shard_map/all_gather | solution.py:41
  367.7 16.7 %all_gather.14 = f32[128,1,4,8,32]{4,3,2,1,0:T(8,128)} all-gather(f32[32,1,4,8,32]{4,3,2,1,0:T(8,128)S(1)} %all_gather.13), channel_id=1, replica_groups=mesh['tm_0'=8,'tm_1'=2,'space_0'=4,'space_1'=4] {'space_1'}, dimensions={0}, use_global_device_ids=true | all-gather | bytes 655360 | tf_op jit(solution)/shard_map/all_gather | solution.py:41
  402.3 5.4 %copy.511 = f32[256,1,4,8,32]{4,3,2,0,1:T(8,128)} copy(f32[256,1,4,8,32]{0,4,3,2,1:T(8,128)} %all-gather.3.cloned.1.call-done) | data formatting | bytes 2097152 | tf_op jit(solution)/shard_map/all_gather | solution.py:41
  (472 shorter events, 286.9 us)
Async XLA Ops:
  6.5 395.8 %all-gather.3.cloned.1.call-start = ((), (), s32[]{:S(2)}) async-start(), calls=%async_computation | async-start | bytes 1572864 | tf_op jit(solution)/shard_map/all_gather | solution.py:41
  7.5 50.2 %collective-permute-start = (f32[2,32,512]{2,1,0:T(8,128)S(1)}, f32[2,32,512]{2,1,0:T(8,128)S(1)}, u32[]{:S(2)}, u32[]{:S(2)}) collective-permute-start(f32[2,32,512]{2,1,0:T(8,128)S(1)} %get-tuple-element.232), channel_id=1, source_target_pairs={{0,16},{16,32},{32,48},{48,64},{64,80},{80,96},{96,112},{112,128},... | collective-permute-start | bytes 393224 | tf_op jit(solution)/shard_map/ppermute | solution.py:29
  10.3 47.2 %collective-permute-start.3 = (f32[5,7,512]{2,1,0:T(8,128)S(1)}, f32[5,7,512]{2,1,0:T(8,128)S(1)}, u32[]{:S(2)}, u32[]{:S(2)}) collective-permute-start(f32[5,7,512]{2,1,0:T(8,128)S(1)} %get-tuple-element.289), channel_id=1, source_target_pairs={{0,1},{1,2},{2,3},{3,4},{4,5},{5,6},{6,7},{7,8},{8,9},{9,10},{10,1... | collective-permute-start | bytes 215048 | tf_op jit(solution)/shard_map/ppermute | solution.py:18
  13.8 43.8 %collective-permute-start.4 = (f32[5,7,512]{2,1,0:T(8,128)S(1)}, f32[5,7,512]{2,1,0:T(8,128)S(1)}, u32[]{:S(2)}, u32[]{:S(2)}) collective-permute-start(f32[5,7,512]{2,1,0:T(8,128)S(1)} %get-tuple-element.290), channel_id=1, source_target_pairs={{1,0},{2,1},{3,2},{4,3},{5,4},{6,5},{7,6},{8,7},{9,8},{10,9},{11,1... | collective-permute-start | bytes 215048 | tf_op jit(solution)/shard_map/ppermute | solution.py:21
  57.8 7.8 %collective-permute-start.1 = (f32[2,2,7,512]{3,1,2,0:T(2,128)S(1)}, f32[2,2,7,512]{3,1,2,0:T(2,128)S(1)}, u32[]{:S(2)}, u32[]{:S(2)}) collective-permute-start(f32[2,2,7,512]{3,1,2,0:T(2,128)S(1)} %copy.483), channel_id=1, source_target_pairs={{0,1},{1,2},{2,3},{3,4},{4,5},{5,6},{6,7},{7,8},{8,9},{9,10},{10,1... | collective-permute-start | bytes 172040 | tf_op jit(solution)/shard_map/ppermute | solution.py:18
  63.4 8.2 %collective-permute-start.2 = (f32[2,2,7,512]{3,1,2,0:T(2,128)S(1)}, f32[2,2,7,512]{3,1,2,0:T(2,128)S(1)}, u32[]{:S(2)}, u32[]{:S(2)}) collective-permute-start(f32[2,2,7,512]{3,1,2,0:T(2,128)S(1)} %copy.484), channel_id=1, source_target_pairs={{1,0},{2,1},{3,2},{4,3},{5,4},{6,5},{7,6},{8,7},{9,8},{10,9},{11,1... | collective-permute-start | bytes 172040 | tf_op jit(solution)/shard_map/ppermute | solution.py:21
  75.8 20.3 %collective-permute-start.5 = (f32[2,2,1,512]{3,1,2,0:T(2,128)S(1)}, f32[2,2,1,512]{3,1,2,0:T(2,128)S(1)}, u32[]{:S(2)}, u32[]{:S(2)}) collective-permute-start(f32[2,2,1,512]{3,1,2,0:T(2,128)S(1)} %copy.487), channel_id=1, source_target_pairs={{0,1},{1,2},{2,3},{3,4},{4,5},{5,6},{6,7},{7,8},{8,9},{9,10},{10,1... | collective-permute-start | bytes 24584 | tf_op jit(solution)/shard_map/ppermute | solution.py:18
  77.7 18.4 %collective-permute-start.6 = (f32[2,2,1,512]{3,1,2,0:T(2,128)S(1)}, f32[2,2,1,512]{3,1,2,0:T(2,128)S(1)}, u32[]{:S(2)}, u32[]{:S(2)}) collective-permute-start(f32[2,2,1,512]{3,1,2,0:T(2,128)S(1)} %copy.489), channel_id=1, source_target_pairs={{1,0},{2,1},{3,2},{4,3},{5,4},{6,5},{7,6},{8,7},{9,8},{10,9},{11,1... | collective-permute-start | bytes 24584 | tf_op jit(solution)/shard_map/ppermute | solution.py:21
  124.8 41.0 %collective-permute-start.10 = (f32[2,32,512]{2,1,0:T(8,128)S(1)}, f32[2,32,512]{2,1,0:T(8,128)S(1)}, u32[]{:S(2)}, u32[]{:S(2)}) collective-permute-start(f32[2,32,512]{2,1,0:T(8,128)S(1)} %bitcast.176), channel_id=1, source_target_pairs={{0,16},{16,32},{32,48},{48,64},{64,80},{80,96},{96,112},{112,128},... | collective-permute-start | bytes 393224 | tf_op jit(solution)/shard_map/ppermute | solution.py:29
  129.3 36.4 %collective-permute-start.8 = (f32[2,2,256]{2,1,0:T(2,128)S(1)}, f32[2,2,256]{2,1,0:T(2,128)S(1)}, u32[]{:S(2)}, u32[]{:S(2)}) collective-permute-start(f32[2,2,256]{2,1,0:T(2,128)S(1)} %get-tuple-element.375), channel_id=1, source_target_pairs={{0,1},{1,2},{2,3},{3,4},{4,5},{5,6},{6,7},{7,8},{8,9},{9,10},{10,1... | collective-permute-start | bytes 12296 | tf_op jit(solution)/shard_map/ppermute | solution.py:18
  133.3 32.4 %collective-permute-start.9 = (f32[2,2,256]{2,1,0:T(2,128)S(1)}, f32[2,2,256]{2,1,0:T(2,128)S(1)}, u32[]{:S(2)}, u32[]{:S(2)}) collective-permute-start(f32[2,2,256]{2,1,0:T(2,128)S(1)} %get-tuple-element.376), channel_id=1, source_target_pairs={{1,0},{2,1},{3,2},{4,3},{5,4},{6,5},{7,6},{8,7},{9,8},{10,9},{11,1... | collective-permute-start | bytes 12296 | tf_op jit(solution)/shard_map/ppermute | solution.py:21
  180.2 16.1 %collective-permute-start.15 = (f32[2,2,1,256]{3,2,1,0:T(1,128)S(1)}, f32[2,2,1,256]{3,2,1,0:T(1,128)S(1)}, u32[]{:S(2)}, u32[]{:S(2)}) collective-permute-start(f32[2,2,1,256]{3,2,1,0:T(1,128)S(1)} %get-tuple-element.342), channel_id=1, source_target_pairs={{0,1},{1,2},{2,3},{3,4},{4,5},{5,6},{6,7},{7,8},{8,9},{9,10},{10,1... | collective-permute-start | bytes 12296 | tf_op jit(solution)/shard_map/ppermute | solution.py:18
  186.3 10.0 %collective-permute-start.16 = (f32[2,2,1,256]{3,2,1,0:T(1,128)S(1)}, f32[2,2,1,256]{3,2,1,0:T(1,128)S(1)}, u32[]{:S(2)}, u32[]{:S(2)}) collective-permute-start(f32[2,2,1,256]{3,2,1,0:T(1,128)S(1)} %get-tuple-element.343), channel_id=1, source_target_pairs={{1,0},{2,1},{3,2},{4,3},{5,4},{6,5},{7,6},{8,7},{9,8},{10,9},{11,1... | collective-permute-start | bytes 12296 | tf_op jit(solution)/shard_map/ppermute | solution.py:21
  188.3 8.3 %collective-permute-start.11 = (f32[2,2,7,512]{3,1,2,0:T(2,128)S(1)}, f32[2,2,7,512]{3,1,2,0:T(2,128)S(1)}, u32[]{:S(2)}, u32[]{:S(2)}) collective-permute-start(f32[2,2,7,512]{3,1,2,0:T(2,128)S(1)} %copy.493), channel_id=1, source_target_pairs={{0,1},{1,2},{2,3},{3,4},{4,5},{5,6},{6,7},{7,8},{8,9},{9,10},{10,1... | collective-permute-start | bytes 172040 | tf_op jit(solution)/shard_map/ppermute | solution.py:18
  194.4 8.2 %collective-permute-start.12 = (f32[2,2,7,512]{3,1,2,0:T(2,128)S(1)}, f32[2,2,7,512]{3,1,2,0:T(2,128)S(1)}, u32[]{:S(2)}, u32[]{:S(2)}) collective-permute-start(f32[2,2,7,512]{3,1,2,0:T(2,128)S(1)} %copy.494), channel_id=1, source_target_pairs={{1,0},{2,1},{3,2},{4,3},{5,4},{6,5},{7,6},{8,7},{9,8},{10,9},{11,1... | collective-permute-start | bytes 172040 | tf_op jit(solution)/shard_map/ppermute | solution.py:21
  208.7 7.7 %collective-permute-start.14 = (f32[2,2,1,512]{3,1,2,0:T(2,128)S(1)}, f32[2,2,1,512]{3,1,2,0:T(2,128)S(1)}, u32[]{:S(2)}, u32[]{:S(2)}) collective-permute-start(f32[2,2,1,512]{3,1,2,0:T(2,128)S(1)} %copy.499), channel_id=1, source_target_pairs={{1,0},{2,1},{3,2},{4,3},{5,4},{6,5},{7,6},{8,7},{9,8},{10,9},{11,1... | collective-permute-start | bytes 24584 | tf_op jit(solution)/shard_map/ppermute | solution.py:21
  249.0 7.8 %collective-permute-start.18 = (f32[9,2,256]{2,1,0:T(2,128)S(1)}, f32[9,2,256]{2,1,0:T(2,128)S(1)}, u32[]{:S(2)}, u32[]{:S(2)}) collective-permute-start(f32[9,2,256]{2,1,0:T(2,128)S(1)} %get-tuple-element.301), channel_id=1, source_target_pairs={{1,0},{2,1},{3,2},{4,3},{5,4},{6,5},{7,6},{8,7},{9,8},{10,9},{11,1... | collective-permute-start | bytes 55304 | tf_op jit(solution)/shard_map/ppermute | solution.py:21
  265.5 7.6 %collective-permute-start.21 = (f32[2,2,256]{2,1,0:T(2,128)S(1)}, f32[2,2,256]{2,1,0:T(2,128)S(1)}, u32[]{:S(2)}, u32[]{:S(2)}) collective-permute-start(f32[2,2,256]{2,1,0:T(2,128)S(1)} %get-tuple-element.372), channel_id=1, source_target_pairs={{1,0},{2,1},{3,2},{4,3},{5,4},{6,5},{7,6},{8,7},{9,8},{10,9},{11,1... | collective-permute-start | bytes 12296 | tf_op jit(solution)/shard_map/ppermute | solution.py:21
  318.3 11.1 %collective-permute-start.30 = (f32[4,8,32]{2,1,0:T(8,128)S(1)}, f32[4,8,32]{2,1,0:T(8,128)S(1)}, u32[]{:S(2)}, u32[]{:S(2)}) collective-permute-start(f32[4,8,32]{2,1,0:T(8,128)S(1)} %get-tuple-element.387), channel_id=1, source_target_pairs={{48,0},{64,16},{80,32},{96,48},{112,64},{128,80},{144,96},{160,112... | collective-permute-start | bytes 12296 | tf_op jit(solution)/shard_map/ppermute | solution.py:29
  320.3 9.2 %collective-permute-start.31 = (f32[4,8,32]{2,1,0:T(8,128)S(1)}, f32[4,8,32]{2,1,0:T(8,128)S(1)}, u32[]{:S(2)}, u32[]{:S(2)}) collective-permute-start(f32[4,8,32]{2,1,0:T(8,128)S(1)} %get-tuple-element.386), channel_id=1, source_target_pairs={{32,0},{48,16},{64,32},{80,48},{96,64},{112,80},{128,96},{144,112}... | collective-permute-start | bytes 12296 | tf_op jit(solution)/shard_map/ppermute | solution.py:29
  390.2 7.7 %collective-permute-start.29 = (f32[7,4,128]{2,1,0:T(4,128)S(1)}, f32[7,4,128]{2,1,0:T(4,128)S(1)}, u32[]{:S(2)}, u32[]{:S(2)}) collective-permute-start(f32[7,4,128]{2,1,0:T(4,128)S(1)} %get-tuple-element.378), channel_id=1, source_target_pairs={{1,0},{2,1},{3,2},{4,3},{5,4},{6,5},{7,6},{8,7},{9,8},{10,9},{11,1... | collective-permute-start | bytes 43016 | tf_op jit(solution)/shard_map/ppermute | solution.py:21
  430.4 7.6 %collective-permute-start.35 = (f32[2,2,256]{2,1,0:T(2,128)S(1)}, f32[2,2,256]{2,1,0:T(2,128)S(1)}, u32[]{:S(2)}, u32[]{:S(2)}) collective-permute-start(f32[2,2,256]{2,1,0:T(2,128)S(1)} %get-tuple-element.361), channel_id=1, source_target_pairs={{1,0},{2,1},{3,2},{4,3},{5,4},{6,5},{7,6},{8,7},{9,8},{10,9},{11,1... | collective-permute-start | bytes 12296 | tf_op jit(solution)/shard_map/ppermute | solution.py:21
  479.9 7.6 %collective-permute-start.44 = (f32[2,2,256]{2,1,0:T(2,128)S(1)}, f32[2,2,256]{2,1,0:T(2,128)S(1)}, u32[]{:S(2)}, u32[]{:S(2)}) collective-permute-start(f32[2,2,256]{2,1,0:T(2,128)S(1)} %get-tuple-element.355), channel_id=1, source_target_pairs={{1,0},{2,1},{3,2},{4,3},{5,4},{6,5},{7,6},{8,7},{9,8},{10,9},{11,1... | collective-permute-start | bytes 12296 | tf_op jit(solution)/shard_map/ppermute | solution.py:21
  498.0 8.2 %collective-permute-start.47 = (f32[2,2,7,512]{3,1,2,0:T(2,128)S(1)}, f32[2,2,7,512]{3,1,2,0:T(2,128)S(1)}, u32[]{:S(2)}, u32[]{:S(2)}) collective-permute-start(f32[2,2,7,512]{3,1,2,0:T(2,128)S(1)} %copy.524), channel_id=1, source_target_pairs={{1,0},{2,1},{3,2},{4,3},{5,4},{6,5},{7,6},{8,7},{9,8},{10,9},{11,1... | collective-permute-start | bytes 172040 | tf_op jit(solution)/shard_map/ppermute | solution.py:21
  (31 other events, 194.2 us)
Sparse Core Ops, SparseCore 0:
  388.0 14.2 all-gather.2
where the time goes:
time: 528 us; the launch traced here: 520 us
  local copies, waits for them, and re-layouts  169 us (32%)
  starting transfers between devices  135 us (26%)
  waiting for transfers between devices  87.7 us (17%)
  other arithmetic  56.9 us (11%)
  blocking collectives  54.8 us (10%)
  between operations  16.5 us (3%)
    reshape x8, local copies, waits for them, and re-layouts, coarsen(): blocks = field.reshape(shape[:-2] + (shape[-2] // 2, 2, shape[-1] // 2, 2))  68.5 us
    ppermute x17, starting transfers between devices, padded_2(): lax.ppermute(lax.slice_in_dim(block, 0, width, axis=dim), axis, backward)  56.9 us
    all_gather x3, blocking collectives, gather_in_order(): parts = lax.all_gather(parts, axes[k], axis=0, tiled=True)  54.8 us
    ppermute x17, waiting for transfers between devices, padded_2(): lax.ppermute(lax.slice_in_dim(block, 0, width, axis=dim), axis, backward)  51.3 us
    ppermute x17, starting transfers between devices, padded_2(): lax.ppermute(lax.slice_in_dim(block, block.shape[dim] - width, None, axis...  49.9 us
    reduce_sum x15, other arithmetic, coarsen(): return blocks.mean(axis=(-3, -1))  38.5 us
    ppermute x14, waiting for transfers between devices, shifted(): return lax.ppermute(block, axis, route)  32 us
    another operation x4, local copies, waits for them, and re-layouts, advance(): return jnp.stack([next_first, next_second], axis=-3)  30.1 us
  transfers between devices with their start and end apart: 49, of which 22 were waited for; matrix products, arithmetic and copies ran while one was open for 20% of the time, Pallas kernels for 0%

commit v1 on v0

--- a/solution.py
+++ b/solution.py
@@ -38,7 +38,11 @@
 def gather_in_order(x, axes, turns):
     parts = x[None]
     for k in turns:
-        parts = lax.all_gather(parts, axes[k], axis=0, tiled=True)
+        buf = axes[k]
+        x_new = lax.axis_size(buf)
+        moved = jnp.stack(x_new * [parts], axis=0)
+        s_next = lax.all_to_all(moved, axis_name=buf, split_axis=0, concat_axis=0)
+        parts = jnp.concatenate(s_next, 0)
     carried = [lax.axis_size(axes[k]) for k in reversed(turns)]
     parts = parts.reshape(*carried, *x.shape)
     turned = sorted(range(len(turns)), key=lambda place: turns[len(turns) - 1 - place])

time: 528 us -> 499 us (0.945)
  blocking collectives: 54.8 us -> 4.81 us
  starting transfers between devices: 135 us -> 154 us
  between operations: 16.5 us -> 3.12 us
  local copies, waits for them, and re-layouts: 169 us -> 176 us
    all_gather x3 -> x0, blocking collectives: 54.8 us -> none  [gather_in_order(): parts = lax.all_gather(parts, axes[k], axis=0, tiled=True)]
    all_to_all x0 -> x3, starting transfers between devices: none -> 18.8 us  [gather_in_order(): s_next = lax.all_to_all(moved, axis_name=buf, split_axis=0, concat_axis=0)]
    all_to_all x0 -> x3, waiting for transfers between devices: none -> 13 us  [gather_in_order(): s_next = lax.all_to_all(moved, axis_name=buf, split_axis=0, concat_axis=0)]
    all_gather x2 -> x0, local copies, waits for them, and re-layouts: 8.86 us -> none  [gather_in_order(): parts = lax.all_gather(parts, axes[k], axis=0, tiled=True)]
    unnamed x28 -> x36, local copies, waits for them, and re-layouts: 1.56 us -> 10 us
    ppermute x17, waiting for transfers between devices: 51.3 us -> 44.6 us  [padded_2(): lax.ppermute(lax.slice_in_dim(block, 0, width, axis=dim), axis, backward)]
  transfers between devices with their start and end apart: 49 -> 51, of which waited for: 22 -> 22; matrix products, arithmetic and copies ran while one was open for 20% -> 21% of each run, Pallas kernels for 0% -> 0%
where the time goes in v1:
time: 499 us; the launch traced here: 490 us
  local copies, waits for them, and re-layouts  176 us (35%)
  starting transfers between devices  154 us (31%)
  waiting for transfers between devices  91.4 us (18%)
  other arithmetic  60.9 us (12%)
    reshape x8, local copies, waits for them, and re-layouts, coarsen(): blocks = field.reshape(shape[:-2] + (shape[-2] // 2, 2, shape[-1] // 2, 2))  68.4 us
    ppermute x17, starting transfers between devices, padded_2(): lax.ppermute(lax.slice_in_dim(block, 0, width, axis=dim), axis, backward)  54.5 us
    ppermute x17, starting transfers between devices, padded_2(): lax.ppermute(lax.slice_in_dim(block, block.shape[dim] - width, None, axis...  52.3 us
    ppermute x17, waiting for transfers between devices, padded_2(): lax.ppermute(lax.slice_in_dim(block, 0, width, axis=dim), axis, backward)  44.6 us
    reduce_sum x15, other arithmetic, coarsen(): return blocks.mean(axis=(-3, -1))  38.5 us
    ppermute x14, waiting for transfers between devices, shifted(): return lax.ppermute(block, axis, route)  33.8 us
    another operation x4, local copies, waits for them, and re-layouts, advance(): return jnp.stack([next_first, next_second], axis=-3)  30 us
    another operation x4, local copies, waits for them, and re-layouts, local(): ends = jnp.stack([series[SPAN - 1], series[-1]])  29.9 us
  transfers between devices with their start and end apart: 51, of which 22 were waited for; matrix products, arithmetic and copies ran while one was open for 21% of the time, Pallas kernels for 0%

profile of v1, /device:TPU:134, one launch (start us, length us, event | category | flops | bytes accessed | tf_op | source)
XLA Modules:
  0.0 490.0 jit_solution(2194052150943166635)
XLA Ops:
  10.6 6.4 %reshape.432 = f32[16,2,256,2]{3,2,1,0:T(8,128)} reshape(f32[32,512]{1,0:T(8,128)} %param.21) | data formatting | bytes 131072 | tf_op jit(solution)/shard_map/reshape | solution.py:58
  17.0 5.5 %reshape.433 = f32[16,2,256,2]{3,2,1,0:T(8,128)} reshape(f32[32,512]{1,0:T(8,128)S(1)} %copy-done.4) | data formatting | bytes 131072 | tf_op jit(solution)/shard_map/reshape | solution.py:58
  22.5 5.6 %reshape.434 = f32[16,2,256,2]{3,2,1,0:T(8,128)} reshape(f32[32,512]{1,0:T(8,128)S(1)} %copy-done.3) | data formatting | bytes 131072 | tf_op jit(solution)/shard_map/reshape | solution.py:58
  28.1 9.8 %reshape.431 = f32[2,16,2,256,2]{4,3,2,1,0:T(8,128)} reshape(f32[2,32,512]{2,1,0:T(8,128)S(1)} %copy-done.1) | data formatting | bytes 262144 | tf_op jit(solution)/shard_map/reshape | solution.py:58
  51.2 5.5 %collective-permute-start.1 = (f32[2,2,7,512]{3,1,2,0:T(2,128)S(1)}, f32[2,2,7,512]{3,1,2,0:T(2,128)S(1)}, u32[]{:S(2)}, u32[]{:S(2)}) collective-permute-start(f32[2,2,7,512]{3,1,2,0:T(2,128)S(1)} %copy.483), channel_id=1, source_target_pairs={{0,1},{1,2},{2,3},{3,4},{4,5},{5,6},{6,7},{7,8},{8,9},{9,10},{10,1... | collective-permute-start | bytes 172040 | tf_op jit(solution)/shard_map/ppermute | solution.py:18
  59.0 6.0 %collective-permute-done.2 = f32[2,2,7,512]{3,1,2,0:T(2,128)S(1)} collective-permute-done((f32[2,2,7,512]{3,1,2,0:T(2,128)S(1)}, f32[2,2,7,512]{3,1,2,0:T(2,128)S(1)}, u32[]{:S(2)}, u32[]{:S(2)}) %collective-permute-start.2) | collective-permute-done | bytes 57376 | tf_op jit(solution)/shard_map/ppermute | solution.py:21
  75.1 9.8 %reshape.429 = f32[2,16,2,256,2]{4,3,2,1,0:T(8,128)} reshape(f32[2,32,512]{2,1,0:T(8,128)S(1)} %copy-done.2) | data formatting | bytes 262144 | tf_op jit(solution)/shard_map/reshape | solution.py:58
  90.0 18.1 %reshape.430 = f32[2,2,16,2,256,2]{5,4,3,2,1,0:T(8,128)} reshape(f32[2,2,32,512]{3,2,1,0:T(8,128)S(1)} %pad_maximum_fusion.5) | data formatting | bytes 524288 | tf_op jit(solution)/shard_map/reshape | solution.py:58
  108.1 8.0 %reduce_sum.136 = f32[2,2,16,256]{3,2,1,0:T(8,128)S(1)} reduce(f32[2,2,16,2,256,2]{5,4,3,2,1,0:T(8,128)} %reshape.430, f32[]{:T(128)} %constant.259.clone.1), dimensions={3,5}, to_apply=%region_1.2 | reduce | flops 49152 | bytes 327684 | tf_op jit(solution)/shard_map/reduce_sum | solution.py:59
  129.1 9.8 %stack.361 = f32[1,2,16,2,256,2]{5,4,3,2,1,0:T(8,128)} reshape(f32[1,2,32,512]{3,2,1,0:T(8,128)S(1)} %get-tuple-element.295) | data formatting | bytes 262144 | tf_op jit(solution)/shard_map/stack | solution.py:179
  138.9 9.7 %stack.360 = f32[1,2,16,2,256,2]{5,4,3,2,1,0:T(8,128)} reshape(f32[1,2,32,512]{3,2,1,0:T(8,128)S(1)} %get-tuple-element.296) | data formatting | bytes 262144 | tf_op jit(solution)/shard_map/stack | solution.py:179
  148.6 5.2 %copy.505 = f32[1,2,16,2,256,2]{4,2,5,3,1,0:T(8,128)S(1)} copy(f32[1,2,16,2,256,2]{5,4,3,2,1,0:T(8,128)} %stack.360) | data formatting | bytes 262144 | tf_op jit(solution)/shard_map/stack | solution.py:179
  153.8 5.2 %copy.506 = f32[1,2,16,2,256,2]{4,2,5,3,1,0:T(8,128)S(1)} copy(f32[1,2,16,2,256,2]{5,4,3,2,1,0:T(8,128)} %stack.361) | data formatting | bytes 262144 | tf_op jit(solution)/shard_map/stack | solution.py:179
  159.1 9.8 %reshape.435 = f32[2,16,2,256,2]{4,3,2,1,0:T(8,128)} reshape(f32[2,32,512]{2,1,0:T(8,128)S(1)} %broadcast_select_fusion) | data formatting | bytes 262144 | tf_op jit(solution)/shard_map/reshape | solution.py:58
  173.5 6.0 %collective-permute-start.15 = (f32[2,2,1,256]{3,2,1,0:T(1,128)S(1)}, f32[2,2,1,256]{3,2,1,0:T(1,128)S(1)}, u32[]{:S(2)}, u32[]{:S(2)}) collective-permute-start(f32[2,2,1,256]{3,2,1,0:T(1,128)S(1)} %get-tuple-element.342), channel_id=1, source_target_pairs={{0,1},{1,2},{2,3},{3,4},{4,5},{5,6},{6,7},{7,8},{8,9},{9,10},{10,1... | collective-permute-start | bytes 12296 | tf_op jit(solution)/shard_map/ppermute | solution.py:18
  181.5 6.0 %collective-permute-start.11 = (f32[2,2,7,512]{3,1,2,0:T(2,128)S(1)}, f32[2,2,7,512]{3,1,2,0:T(2,128)S(1)}, u32[]{:S(2)}, u32[]{:S(2)}) collective-permute-start(f32[2,2,7,512]{3,1,2,0:T(2,128)S(1)} %copy.493), channel_id=1, source_target_pairs={{0,1},{1,2},{2,3},{3,4},{4,5},{5,6},{6,7},{7,8},{8,9},{9,10},{10,1... | collective-permute-start | bytes 172040 | tf_op jit(solution)/shard_map/ppermute | solution.py:18
  189.8 6.0 %collective-permute-done.12 = f32[2,2,7,512]{3,1,2,0:T(2,128)S(1)} collective-permute-done((f32[2,2,7,512]{3,1,2,0:T(2,128)S(1)}, f32[2,2,7,512]{3,1,2,0:T(2,128)S(1)}, u32[]{:S(2)}, u32[]{:S(2)}) %collective-permute-start.12) | collective-permute-done | bytes 57376 | tf_op jit(solution)/shard_map/ppermute | solution.py:21
  210.1 9.8 %stack.357 = f32[2,1,16,2,256,2]{5,4,3,2,0,1:T(8,128)} reshape(f32[2,1,32,512]{3,2,1,0:T(8,128)S(1)} %get-tuple-element.276) | data formatting | bytes 262144 | tf_op jit(solution)/shard_map/stack | solution.py:88
  225.1 9.8 %stack.358 = f32[2,1,16,2,256,2]{5,4,3,2,0,1:T(8,128)} reshape(f32[2,1,32,512]{3,2,1,0:T(8,128)S(1)} %get-tuple-element.277) | data formatting | bytes 262144 | tf_op jit(solution)/shard_map/stack | solution.py:88
  321.9 7.9 %all-to-all-start = ((f32[8,1,1024]{2,1,0:T(1,128)}), f32[8,1,1024]{2,1,0:T(1,128)S(1)}, u32[]{:S(2)}, u32[]{:S(2)}) async-start(f32[8,1,1024]{2,1,0:T(1,128)} %reshape.443), calls=%async_computation | async-start | bytes 65536 | tf_op jit(solution)/shard_map/all_to_all | solution.py:44
  342.4 6.1 %all-to-all-done.1 = f32[4,1,8192]{2,1,0:T(1,128)S(1)} async-done(((f32[4,1,8192]{2,1,0:T(1,128)}), f32[4,1,8192]{2,1,0:T(1,128)S(1)}, u32[]{:S(2)}, u32[]{:S(2)}) %all-to-all-start.1) | async-done | bytes 131104 | tf_op jit(solution)/shard_map/all_to_all | solution.py:44
  354.2 6.7 %all-to-all-start.2 = ((f32[4,1,32768]{2,1,0:T(1,128)}), f32[4,1,32768]{2,1,0:T(1,128)S(1)}, u32[]{:S(2)}, u32[]{:S(2)}) async-start(f32[4,1,32768]{2,1,0:T(1,128)} %reshape.447), calls=%async_computation.2 | async-start | bytes 1048576 | tf_op jit(solution)/shard_map/all_to_all | solution.py:44
  360.8 6.9 %all-to-all-done.2 = f32[4,1,32768]{2,1,0:T(1,128)S(1)} async-done(((f32[4,1,32768]{2,1,0:T(1,128)}), f32[4,1,32768]{2,1,0:T(1,128)S(1)}, u32[]{:S(2)}, u32[]{:S(2)}) %all-to-all-start.2) | async-done | bytes 524320 | tf_op jit(solution)/shard_map/all_to_all | solution.py:44
  409.2 5.7 %collective-permute-done.35 = f32[2,2,256]{2,1,0:T(2,128)S(1)} collective-permute-done((f32[2,2,256]{2,1,0:T(2,128)S(1)}, f32[2,2,256]{2,1,0:T(2,128)S(1)}, u32[]{:S(2)}, u32[]{:S(2)}) %collective-permute-start.35) | collective-permute-done | bytes 4128 | tf_op jit(solution)/shard_map/ppermute | solution.py:21
  (487 shorter events, 302.7 us)
Async XLA Ops:
  1.0 50.1 %collective-permute-start = (f32[2,32,512]{2,1,0:T(8,128)S(1)}, f32[2,32,512]{2,1,0:T(8,128)S(1)}, u32[]{:S(2)}, u32[]{:S(2)}) collective-permute-start(f32[2,32,512]{2,1,0:T(8,128)S(1)} %get-tuple-element.232), channel_id=1, source_target_pairs={{0,16},{16,32},{32,48},{48,64},{64,80},{80,96},{96,112},{112,128},... | collective-permute-start | bytes 393224 | tf_op jit(solution)/shard_map/ppermute | solution.py:29
  3.8 47.2 %collective-permute-start.3 = (f32[5,7,512]{2,1,0:T(8,128)S(1)}, f32[5,7,512]{2,1,0:T(8,128)S(1)}, u32[]{:S(2)}, u32[]{:S(2)}) collective-permute-start(f32[5,7,512]{2,1,0:T(8,128)S(1)} %get-tuple-element.289), channel_id=1, source_target_pairs={{0,1},{1,2},{2,3},{3,4},{4,5},{5,6},{6,7},{7,8},{8,9},{9,10},{10,1... | collective-permute-start | bytes 215048 | tf_op jit(solution)/shard_map/ppermute | solution.py:18
  7.2 43.8 %collective-permute-start.4 = (f32[5,7,512]{2,1,0:T(8,128)S(1)}, f32[5,7,512]{2,1,0:T(8,128)S(1)}, u32[]{:S(2)}, u32[]{:S(2)}) collective-permute-start(f32[5,7,512]{2,1,0:T(8,128)S(1)} %get-tuple-element.290), channel_id=1, source_target_pairs={{1,0},{2,1},{3,2},{4,3},{5,4},{6,5},{7,6},{8,7},{9,8},{10,9},{11,1... | collective-permute-start | bytes 215048 | tf_op jit(solution)/shard_map/ppermute | solution.py:21
  51.2 7.8 %collective-permute-start.1 = (f32[2,2,7,512]{3,1,2,0:T(2,128)S(1)}, f32[2,2,7,512]{3,1,2,0:T(2,128)S(1)}, u32[]{:S(2)}, u32[]{:S(2)}) collective-permute-start(f32[2,2,7,512]{3,1,2,0:T(2,128)S(1)} %copy.483), channel_id=1, source_target_pairs={{0,1},{1,2},{2,3},{3,4},{4,5},{5,6},{6,7},{7,8},{8,9},{9,10},{10,1... | collective-permute-start | bytes 172040 | tf_op jit(solution)/shard_map/ppermute | solution.py:18
  56.8 8.2 %collective-permute-start.2 = (f32[2,2,7,512]{3,1,2,0:T(2,128)S(1)}, f32[2,2,7,512]{3,1,2,0:T(2,128)S(1)}, u32[]{:S(2)}, u32[]{:S(2)}) collective-permute-start(f32[2,2,7,512]{3,1,2,0:T(2,128)S(1)} %copy.484), channel_id=1, source_target_pairs={{1,0},{2,1},{3,2},{4,3},{5,4},{6,5},{7,6},{8,7},{9,8},{10,9},{11,1... | collective-permute-start | bytes 172040 | tf_op jit(solution)/shard_map/ppermute | solution.py:21
  69.2 20.3 %collective-permute-start.5 = (f32[2,2,1,512]{3,1,2,0:T(2,128)S(1)}, f32[2,2,1,512]{3,1,2,0:T(2,128)S(1)}, u32[]{:S(2)}, u32[]{:S(2)}) collective-permute-start(f32[2,2,1,512]{3,1,2,0:T(2,128)S(1)} %copy.487), channel_id=1, source_target_pairs={{0,1},{1,2},{2,3},{3,4},{4,5},{5,6},{6,7},{7,8},{8,9},{9,10},{10,1... | collective-permute-start | bytes 24584 | tf_op jit(solution)/shard_map/ppermute | solution.py:18
  71.1 18.4 %collective-permute-start.6 = (f32[2,2,1,512]{3,1,2,0:T(2,128)S(1)}, f32[2,2,1,512]{3,1,2,0:T(2,128)S(1)}, u32[]{:S(2)}, u32[]{:S(2)}) collective-permute-start(f32[2,2,1,512]{3,1,2,0:T(2,128)S(1)} %copy.489), channel_id=1, source_target_pairs={{1,0},{2,1},{3,2},{4,3},{5,4},{6,5},{7,6},{8,7},{9,8},{10,9},{11,1... | collective-permute-start | bytes 24584 | tf_op jit(solution)/shard_map/ppermute | solution.py:21
  118.1 41.0 %collective-permute-start.10 = (f32[2,32,512]{2,1,0:T(8,128)S(1)}, f32[2,32,512]{2,1,0:T(8,128)S(1)}, u32[]{:S(2)}, u32[]{:S(2)}) collective-permute-start(f32[2,32,512]{2,1,0:T(8,128)S(1)} %bitcast.184), channel_id=1, source_target_pairs={{0,16},{16,32},{32,48},{48,64},{64,80},{80,96},{96,112},{112,128},... | collective-permute-start | bytes 393224 | tf_op jit(solution)/shard_map/ppermute | solution.py:29
  122.6 36.4 %collective-permute-start.8 = (f32[2,2,256]{2,1,0:T(2,128)S(1)}, f32[2,2,256]{2,1,0:T(2,128)S(1)}, u32[]{:S(2)}, u32[]{:S(2)}) collective-permute-start(f32[2,2,256]{2,1,0:T(2,128)S(1)} %get-tuple-element.375), channel_id=1, source_target_pairs={{0,1},{1,2},{2,3},{3,4},{4,5},{5,6},{6,7},{7,8},{8,9},{9,10},{10,1... | collective-permute-start | bytes 12296 | tf_op jit(solution)/shard_map/ppermute | solution.py:18
  126.7 32.4 %collective-permute-start.9 = (f32[2,2,256]{2,1,0:T(2,128)S(1)}, f32[2,2,256]{2,1,0:T(2,128)S(1)}, u32[]{:S(2)}, u32[]{:S(2)}) collective-permute-start(f32[2,2,256]{2,1,0:T(2,128)S(1)} %get-tuple-element.376), channel_id=1, source_target_pairs={{1,0},{2,1},{3,2},{4,3},{5,4},{6,5},{7,6},{8,7},{9,8},{10,9},{11,1... | collective-permute-start | bytes 12296 | tf_op jit(solution)/shard_map/ppermute | solution.py:21
  173.5 16.1 %collective-permute-start.15 = (f32[2,2,1,256]{3,2,1,0:T(1,128)S(1)}, f32[2,2,1,256]{3,2,1,0:T(1,128)S(1)}, u32[]{:S(2)}, u32[]{:S(2)}) collective-permute-start(f32[2,2,1,256]{3,2,1,0:T(1,128)S(1)} %get-tuple-element.342), channel_id=1, source_target_pairs={{0,1},{1,2},{2,3},{3,4},{4,5},{5,6},{6,7},{7,8},{8,9},{9,10},{10,1... | collective-permute-start | bytes 12296 | tf_op jit(solution)/shard_map/ppermute | solution.py:18
  179.5 10.0 %collective-permute-start.16 = (f32[2,2,1,256]{3,2,1,0:T(1,128)S(1)}, f32[2,2,1,256]{3,2,1,0:T(1,128)S(1)}, u32[]{:S(2)}, u32[]{:S(2)}) collective-permute-start(f32[2,2,1,256]{3,2,1,0:T(1,128)S(1)} %get-tuple-element.343), channel_id=1, source_target_pairs={{1,0},{2,1},{3,2},{4,3},{5,4},{6,5},{7,6},{8,7},{9,8},{10,9},{11,1... | collective-permute-start | bytes 12296 | tf_op jit(solution)/shard_map/ppermute | solution.py:21
  181.5 8.3 %collective-permute-start.11 = (f32[2,2,7,512]{3,1,2,0:T(2,128)S(1)}, f32[2,2,7,512]{3,1,2,0:T(2,128)S(1)}, u32[]{:S(2)}, u32[]{:S(2)}) collective-permute-start(f32[2,2,7,512]{3,1,2,0:T(2,128)S(1)} %copy.493), channel_id=1, source_target_pairs={{0,1},{1,2},{2,3},{3,4},{4,5},{5,6},{6,7},{7,8},{8,9},{9,10},{10,1... | collective-permute-start | bytes 172040 | tf_op jit(solution)/shard_map/ppermute | solution.py:18
  187.6 8.2 %collective-permute-start.12 = (f32[2,2,7,512]{3,1,2,0:T(2,128)S(1)}, f32[2,2,7,512]{3,1,2,0:T(2,128)S(1)}, u32[]{:S(2)}, u32[]{:S(2)}) collective-permute-start(f32[2,2,7,512]{3,1,2,0:T(2,128)S(1)} %copy.494), channel_id=1, source_target_pairs={{1,0},{2,1},{3,2},{4,3},{5,4},{6,5},{7,6},{8,7},{9,8},{10,9},{11,1... | collective-permute-start | bytes 172040 | tf_op jit(solution)/shard_map/ppermute | solution.py:21
  201.9 7.7 %collective-permute-start.14 = (f32[2,2,1,512]{3,1,2,0:T(2,128)S(1)}, f32[2,2,1,512]{3,1,2,0:T(2,128)S(1)}, u32[]{:S(2)}, u32[]{:S(2)}) collective-permute-start(f32[2,2,1,512]{3,1,2,0:T(2,128)S(1)} %copy.499), channel_id=1, source_target_pairs={{1,0},{2,1},{3,2},{4,3},{5,4},{6,5},{7,6},{8,7},{9,8},{10,9},{11,1... | collective-permute-start | bytes 24584 | tf_op jit(solution)/shard_map/ppermute | solution.py:21
  242.2 7.8 %collective-permute-start.18 = (f32[9,2,256]{2,1,0:T(2,128)S(1)}, f32[9,2,256]{2,1,0:T(2,128)S(1)}, u32[]{:S(2)}, u32[]{:S(2)}) collective-permute-start(f32[9,2,256]{2,1,0:T(2,128)S(1)} %get-tuple-element.301), channel_id=1, source_target_pairs={{1,0},{2,1},{3,2},{4,3},{5,4},{6,5},{7,6},{8,7},{9,8},{10,9},{11,1... | collective-permute-start | bytes 55304 | tf_op jit(solution)/shard_map/ppermute | solution.py:21
  290.7 11.5 %collective-permute-start.26 = (f32[2,2,256]{2,1,0:T(2,128)S(1)}, f32[2,2,256]{2,1,0:T(2,128)S(1)}, u32[]{:S(2)}, u32[]{:S(2)}) collective-permute-start(f32[2,2,256]{2,1,0:T(2,128)S(1)} %get-tuple-element.367), channel_id=1, source_target_pairs={{0,1},{1,2},{2,3},{3,4},{4,5},{5,6},{6,7},{7,8},{8,9},{9,10},{10,1... | collective-permute-start | bytes 12296 | tf_op jit(solution)/shard_map/ppermute | solution.py:18
  292.6 9.6 %collective-permute-start.27 = (f32[2,2,256]{2,1,0:T(2,128)S(1)}, f32[2,2,256]{2,1,0:T(2,128)S(1)}, u32[]{:S(2)}, u32[]{:S(2)}) collective-permute-start(f32[2,2,256]{2,1,0:T(2,128)S(1)} %get-tuple-element.368), channel_id=1, source_target_pairs={{1,0},{2,1},{3,2},{4,3},{5,4},{6,5},{7,6},{8,7},{9,8},{10,9},{11,1... | collective-permute-start | bytes 12296 | tf_op jit(solution)/shard_map/ppermute | solution.py:21
  321.9 13.9 %all-to-all-start = ((f32[8,1,1024]{2,1,0:T(1,128)}), f32[8,1,1024]{2,1,0:T(1,128)S(1)}, u32[]{:S(2)}, u32[]{:S(2)}) async-start(f32[8,1,1024]{2,1,0:T(1,128)} %reshape.443), calls=%async_computation | async-start | bytes 65536 | tf_op jit(solution)/shard_map/all_to_all | solution.py:44
  329.8 12.6 %collective-permute-start.28 = (f32[7,4,128]{2,1,0:T(4,128)S(1)}, f32[7,4,128]{2,1,0:T(4,128)S(1)}, u32[]{:S(2)}, u32[]{:S(2)}) collective-permute-start(f32[7,4,128]{2,1,0:T(4,128)S(1)} %get-tuple-element.377), channel_id=1, source_target_pairs={{0,1},{1,2},{2,3},{3,4},{4,5},{5,6},{6,7},{7,8},{8,9},{9,10},{10,1... | collective-permute-start | bytes 43016 | tf_op jit(solution)/shard_map/ppermute | solution.py:18
  333.9 8.5 %collective-permute-start.29 = (f32[7,4,128]{2,1,0:T(4,128)S(1)}, f32[7,4,128]{2,1,0:T(4,128)S(1)}, u32[]{:S(2)}, u32[]{:S(2)}) collective-permute-start(f32[7,4,128]{2,1,0:T(4,128)S(1)} %get-tuple-element.378), channel_id=1, source_target_pairs={{1,0},{2,1},{3,2},{4,3},{5,4},{6,5},{7,6},{8,7},{9,8},{10,9},{11,1... | collective-permute-start | bytes 43016 | tf_op jit(solution)/shard_map/ppermute | solution.py:21
  338.2 10.3 %all-to-all-start.1 = ((f32[4,1,8192]{2,1,0:T(1,128)}), f32[4,1,8192]{2,1,0:T(1,128)S(1)}, u32[]{:S(2)}, u32[]{:S(2)}) async-start(f32[4,1,8192]{2,1,0:T(1,128)} %reshape.445), calls=%async_computation.1 | async-start | bytes 262144 | tf_op jit(solution)/shard_map/all_to_all | solution.py:44
  354.2 13.6 %all-to-all-start.2 = ((f32[4,1,32768]{2,1,0:T(1,128)}), f32[4,1,32768]{2,1,0:T(1,128)S(1)}, u32[]{:S(2)}, u32[]{:S(2)}) async-start(f32[4,1,32768]{2,1,0:T(1,128)} %reshape.447), calls=%async_computation.2 | async-start | bytes 1048576 | tf_op jit(solution)/shard_map/all_to_all | solution.py:44
  474.8 8.2 %collective-permute-start.47 = (f32[2,2,7,512]{3,1,2,0:T(2,128)S(1)}, f32[2,2,7,512]{3,1,2,0:T(2,128)S(1)}, u32[]{:S(2)}, u32[]{:S(2)}) collective-permute-start(f32[2,2,7,512]{3,1,2,0:T(2,128)S(1)} %copy.524), channel_id=1, source_target_pairs={{1,0},{2,1},{3,2},{4,3},{5,4},{6,5},{7,6},{8,7},{9,8},{10,9},{11,1... | collective-permute-start | bytes 172040 | tf_op jit(solution)/shard_map/ppermute | solution.py:21
  (33 other events, 205.2 us)
